TPU v7x, 32 devices: a 4x4x1 block of a 4x4x8 slice. The times are simulated.
32 devices in a mesh: part: 1 (over z), row: 4 (over y), col: 8 (over x, core).
Axes of the slice: x: 4, y: 4, z: 1, core: 2. Of those that a mesh axis runs over, the one named last changes fastest.
The devices are a block of a 4x4x8 slice.
Arguments:
- counts: bfloat16 [16384, 8192], P(('part', 'row'), 'col')
- w_init: float32 [16384, 1024], P(('part', 'row'))
- h_init: float32 [1024, 8192], P(None, ('part', 'col'))
Outputs:
- output 1: float32 [16384, 1024], P(('part', 'row'))
- output 2: float32 [1024, 8192], P(None, ('part', 'col'))
All inputs are finite; a program needn't handle non-finite values.
Results may differ from a plain program's by a relative error of at most 0.001.
Values are sent between devices in bfloat16 or wider.
A program may use at most 768 MiB of HBM per device.

v0:
```python
import jax
import jax.numpy as jnp
from jax import lax
from jax.sharding import PartitionSpec as P

SWEEPS = 4
EPS = 1e-6
CONTRACT_WORDS = (((1,), (1,)), ((), ()))
CONTRACT_DOCS = (((0,), (0,)), ((), ()))


def ratio_block(c_blk, w_bf, h_bf):
    z_blk = jnp.dot(w_bf, h_bf, preferred_element_type=jnp.float32)
    return (c_blk.astype(jnp.float32) / (z_blk + EPS)).astype(jnp.bfloat16)


def local_sweeps(c_blk, w_loc, h_loc):
    for sweep_index in range(SWEEPS):
        h_bf = h_loc.astype(jnp.bfloat16)
        q_blk = ratio_block(c_blk, w_loc.astype(jnp.bfloat16), h_bf)
        a_w = lax.psum(lax.dot_general(q_blk, h_bf, CONTRACT_WORDS, preferred_element_type=jnp.float32), 'col')
        s_h = lax.psum(jnp.sum(h_loc, axis=1), 'col')
        w_loc = w_loc * a_w / s_h
        w_bf = w_loc.astype(jnp.bfloat16)
        q_blk = ratio_block(c_blk, w_bf, h_bf)
        a_h = lax.psum(lax.dot_general(w_bf, q_blk, CONTRACT_DOCS, preferred_element_type=jnp.float32), 'row')
        s_w = lax.psum(jnp.sum(w_loc, axis=0), 'row')
        h_loc = h_loc * a_h / s_w[:, None]
    return w_loc, h_loc


def solution(mesh):
    spec_c = P(('part', 'row'), 'col')
    spec_w = P(('part', 'row'), None)
    spec_h = P(None, ('part', 'col'))
    return jax.shard_map(local_sweeps, mesh=mesh, in_specs=(spec_c, spec_w, spec_h), out_specs=(spec_w, spec_h), check_vma=False)
```

profile of v0, /device:TPU:97, one launch (start us, length us, event | category | flops | bytes accessed | tf_op | source)
XLA Modules:
  0.0 1408.3 jit_solution(5568076472521929195)
XLA Ops:
  7.2 29.7 %fusion.16 = f32[4096,1024]{1,0:T(8,128)} fusion(bf16[4096,1024]{1,0:T(8,128)(2,1)} %param.3, f32[4096,1024]{1,0:T(8,128)} %param.4, f32[1024,1024]{1,0:T(8,128)} %param.5), kind=kOutput, calls=%fused_computation.25 | convolution fusion | flops 17202937856 | bytes 46137344 | tf_op jit(solution)/shard_map/dot_general | solution.py:21
  39.5 13.9 psum.113
  53.5 164.9 %all-reduce.9.cloned.1.call-done = f32[4096,1024]{1,0:T(8,128)} async-done(((f32[4096,1024]{1,0:T(8,128)}), f32[4096,1024]{1,0:T(8,128)}) %all-reduce.9.cloned.1.call-update) | async-done | bytes 16777232 | tf_op jit(solution)/shard_map/psum | solution.py:21
  218.4 18.0 %fusion.88 = (f32[1024]{0:T(1024)S(1)}, f32[4096,1024]{1,0:T(8,128)}) fusion(f32[1024]{0:T(1024)S(1)} %psum.113, f32[4096,1024]{1,0:T(8,128)} %param.4, f32[4096,1024]{1,0:T(8,128)} %all-reduce.9.cloned.1.call-done), kind=kLoop, calls=%fused_computation.70 | loop fusion | flops 12581888 | bytes 50339840 | tf_op jit(solution)/shard_map/reduce_sum | solution.py:27
  236.4 28.2 %fusion.24 = f32[1024,1024]{1,0:T(8,128)} fusion(bf16[4096,1024]{1,0:T(8,128)(2,1)} %param.3, f32[4096,1024]{1,0:T(8,128)} %get-tuple-element.15, f32[1024,1024]{1,0:T(8,128)} %param.5), kind=kOutput, calls=%fused_computation.29 | convolution fusion | flops 17206083584 | bytes 33554432 | tf_op jit(solution)/shard_map/dot_general | solution.py:26
  264.7 8.7 psum.115
  273.4 79.2 %all-reduce.11.cloned.1.call-done = f32[1024,1024]{1,0:T(8,128)} async-done(((f32[1024,1024]{1,0:T(8,128)}), f32[1024,1024]{1,0:T(8,128)}) %all-reduce.11.cloned.1.call-update) | async-done | bytes 4194320 | tf_op jit(solution)/shard_map/psum | solution.py:26
  352.6 6.0 fusion.87
  358.6 29.5 %fusion.14 = f32[4096,1024]{1,0:T(8,128)} fusion(bf16[4096,1024]{1,0:T(8,128)(2,1)} %param.3, f32[4096,1024]{1,0:T(8,128)} %get-tuple-element.15, f32[1024,1024]{1,0:T(8,128)} %get-tuple-element.13), kind=kOutput, calls=%fused_computation.24 | convolution fusion | flops 17202937856 | bytes 46137344 | tf_op jit(solution)/shard_map/dot_general | solution.py:21
  388.3 12.8 psum.117
  401.1 164.5 %all-reduce.13.cloned.1.call-done = f32[4096,1024]{1,0:T(8,128)} async-done(((f32[4096,1024]{1,0:T(8,128)}), f32[4096,1024]{1,0:T(8,128)}) %all-reduce.13.cloned.1.call-update) | async-done | bytes 16777232 | tf_op jit(solution)/shard_map/psum | solution.py:21
  565.6 18.0 %fusion.86 = (f32[1024]{0:T(1024)S(1)}, f32[4096,1024]{1,0:T(8,128)}) fusion(f32[1024]{0:T(1024)S(1)} %psum.117, f32[4096,1024]{1,0:T(8,128)} %get-tuple-element.15, f32[4096,1024]{1,0:T(8,128)} %all-reduce.13.cloned.1.call-done), kind=kLoop, calls=%fused_computation.68 | loop fusion | flops 12581888 | bytes 50339840 | tf_op jit(solution)/shard_map/reduce_sum | solution.py:27
  583.6 28.1 %fusion.22 = f32[1024,1024]{1,0:T(8,128)} fusion(bf16[4096,1024]{1,0:T(8,128)(2,1)} %param.3, f32[4096,1024]{1,0:T(8,128)} %get-tuple-element.11, f32[1024,1024]{1,0:T(8,128)} %get-tuple-element.13), kind=kOutput, calls=%fused_computation.28 | convolution fusion | flops 17206083584 | bytes 33554432 | tf_op jit(solution)/shard_map/dot_general | solution.py:26
  611.9 8.7 psum.119
  620.6 79.2 %all-reduce.15.cloned.1.call-done = f32[1024,1024]{1,0:T(8,128)} async-done(((f32[1024,1024]{1,0:T(8,128)}), f32[1024,1024]{1,0:T(8,128)}) %all-reduce.15.cloned.1.call-update) | async-done | bytes 4194320 | tf_op jit(solution)/shard_map/psum | solution.py:26
  699.8 6.0 fusion.85
  705.8 29.5 %fusion.12 = f32[4096,1024]{1,0:T(8,128)} fusion(bf16[4096,1024]{1,0:T(8,128)(2,1)} %param.3, f32[4096,1024]{1,0:T(8,128)} %get-tuple-element.11, f32[1024,1024]{1,0:T(8,128)} %get-tuple-element.9), kind=kOutput, calls=%fused_computation.23 | convolution fusion | flops 17202937856 | bytes 46137344 | tf_op jit(solution)/shard_map/dot_general | solution.py:21
  735.5 12.8 psum.121
  748.3 164.5 %all-reduce.17.cloned.1.call-done = f32[4096,1024]{1,0:T(8,128)} async-done(((f32[4096,1024]{1,0:T(8,128)}), f32[4096,1024]{1,0:T(8,128)}) %all-reduce.17.cloned.1.call-update) | async-done | bytes 16777232 | tf_op jit(solution)/shard_map/psum | solution.py:21
  912.8 18.0 %fusion.84 = (f32[1024]{0:T(1024)S(1)}, f32[4096,1024]{1,0:T(8,128)}) fusion(f32[1024]{0:T(1024)S(1)} %psum.121, f32[4096,1024]{1,0:T(8,128)} %get-tuple-element.11, f32[4096,1024]{1,0:T(8,128)} %all-reduce.17.cloned.1.call-done), kind=kLoop, calls=%fused_computation.66 | loop fusion | flops 12581888 | bytes 50339840 | tf_op jit(solution)/shard_map/reduce_sum | solution.py:27
  930.9 28.1 %fusion.20 = f32[1024,1024]{1,0:T(8,128)} fusion(bf16[4096,1024]{1,0:T(8,128)(2,1)} %param.3, f32[4096,1024]{1,0:T(8,128)} %get-tuple-element.7, f32[1024,1024]{1,0:T(8,128)} %get-tuple-element.9), kind=kOutput, calls=%fused_computation.27 | convolution fusion | flops 17206083584 | bytes 33554432 | tf_op jit(solution)/shard_map/dot_general | solution.py:26
  959.1 8.7 psum.123
  967.9 79.2 %all-reduce.19.cloned.1.call-done = f32[1024,1024]{1,0:T(8,128)} async-done(((f32[1024,1024]{1,0:T(8,128)}), f32[1024,1024]{1,0:T(8,128)}) %all-reduce.19.cloned.1.call-update) | async-done | bytes 4194320 | tf_op jit(solution)/shard_map/psum | solution.py:26
  1047.0 6.0 fusion.83
  1053.0 29.5 %fusion.10 = f32[4096,1024]{1,0:T(8,128)} fusion(bf16[4096,1024]{1,0:T(8,128)(2,1)} %param.3, f32[4096,1024]{1,0:T(8,128)} %get-tuple-element.7, f32[1024,1024]{1,0:T(8,128)} %get-tuple-element.5), kind=kOutput, calls=%fused_computation.22 | convolution fusion | flops 17202937856 | bytes 46137344 | tf_op jit(solution)/shard_map/dot_general | solution.py:21
  1082.7 12.8 psum.125
  1095.5 164.5 %all-reduce.21.cloned.1.call-done = f32[4096,1024]{1,0:T(8,128)} async-done(((f32[4096,1024]{1,0:T(8,128)}), f32[4096,1024]{1,0:T(8,128)}) %all-reduce.21.cloned.1.call-update) | async-done | bytes 16777232 | tf_op jit(solution)/shard_map/psum | solution.py:21
  1260.0 18.0 %fusion.82 = (f32[1024]{0:T(1024)S(1)}, f32[4096,1024]{1,0:T(8,128)}) fusion(f32[1024]{0:T(1024)S(1)} %psum.125, f32[4096,1024]{1,0:T(8,128)} %get-tuple-element.7, f32[4096,1024]{1,0:T(8,128)} %all-reduce.21.cloned.1.call-done), kind=kLoop, calls=%fused_computation.64 | loop fusion | flops 12581888 | bytes 50339840 | tf_op jit(solution)/shard_map/reduce_sum | solution.py:27
  1278.1 28.1 %fusion.18 = f32[1024,1024]{1,0:T(8,128)} fusion(bf16[4096,1024]{1,0:T(8,128)(2,1)} %param.3, f32[4096,1024]{1,0:T(8,128)} %get-tuple-element.3, f32[1024,1024]{1,0:T(8,128)} %get-tuple-element.5), kind=kOutput, calls=%fused_computation.26 | convolution fusion | flops 17206083584 | bytes 33554432 | tf_op jit(solution)/shard_map/dot_general | solution.py:26
  1306.3 8.5 psum.127
  1314.8 79.5 %all-reduce.23.cloned.1.call-done = f32[1024,1024]{1,0:T(8,128)} async-done(((f32[1024,1024]{1,0:T(8,128)}), f32[1024,1024]{1,0:T(8,128)}) %all-reduce.23.cloned.1.call-update) | async-done | bytes 4194320 | tf_op jit(solution)/shard_map/psum | solution.py:26
  1394.3 6.7 multiply_divide_fusion.4
  (17 shorter events, 3.4 us)
Async XLA Ops:
  7.2 211.2 %all-reduce.9.cloned.1.call-start = ((), (), s32[]{:S(2)}) async-start(), calls=%async_computation | async-start | bytes 33554432 | tf_op jit(solution)/shard_map/psum | solution.py:21
  37.0 315.6 %all-reduce.11.cloned.1.call-start = ((), (), s32[]{:S(2)}) async-start(), calls=%async_computation.1 | async-start | bytes 8388608 | tf_op jit(solution)/shard_map/psum | solution.py:26
  264.6 301.0 %all-reduce.13.cloned.1.call-start = ((), (), s32[]{:S(2)}) async-start(), calls=%async_computation.2 | async-start | bytes 33554432 | tf_op jit(solution)/shard_map/psum | solution.py:21
  388.2 311.6 %all-reduce.15.cloned.1.call-start = ((), (), s32[]{:S(2)}) async-start(), calls=%async_computation.3 | async-start | bytes 8388608 | tf_op jit(solution)/shard_map/psum | solution.py:26
  611.8 301.0 %all-reduce.17.cloned.1.call-start = ((), (), s32[]{:S(2)}) async-start(), calls=%async_computation.4 | async-start | bytes 33554432 | tf_op jit(solution)/shard_map/psum | solution.py:21
  735.4 311.6 %all-reduce.19.cloned.1.call-start = ((), (), s32[]{:S(2)}) async-start(), calls=%async_computation.5 | async-start | bytes 8388608 | tf_op jit(solution)/shard_map/psum | solution.py:26
  959.0 301.0 %all-reduce.21.cloned.1.call-start = ((), (), s32[]{:S(2)}) async-start(), calls=%async_computation.6 | async-start | bytes 33554432 | tf_op jit(solution)/shard_map/psum | solution.py:21
  1082.6 311.6 %all-reduce.23.cloned.1.call-start = ((), (), s32[]{:S(2)}) async-start(), calls=%async_computation.7 | async-start | bytes 8388608 | tf_op jit(solution)/shard_map/psum | solution.py:26
Sparse Core Ops, SparseCore 0:
  37.1 181.1 all-reduce.8
  264.7 87.8 all-reduce.10
  388.3 177.2 all-reduce.12
  611.9 87.8 all-reduce.14
  735.5 177.2 all-reduce.16
  959.2 87.8 all-reduce.18
  1082.7 177.2 all-reduce.20
  1306.4 87.8 all-reduce.22
where the time goes:
time: 1420 us; the launch traced here: 1410 us
  waiting for transfers between devices  976 us (69%)
  matrix products  231 us (16%)
  other arithmetic  99.2 us (7%)
  blocking collectives  87.1 us (6%)
  between operations  14.6 us (1%)
    psum x4, waiting for transfers between devices, local_sweeps(): lax.psum(lax.dot_general(q_blk, h_bf, CONTRACT_WORDS, preferred_element_t...  658 us
    psum x4, waiting for transfers between devices, local_sweeps(): lax.psum(lax.dot_general(w_bf, q_blk, CONTRACT_DOCS, preferred_element_ty...  317 us
    dot_general x4, matrix products, local_sweeps(): lax.dot_general(q_blk, h_bf, CONTRACT_WORDS, preferred_element_type=jnp.f...  118 us
    dot_general x4, matrix products, local_sweeps(): lax.dot_general(w_bf, q_blk, CONTRACT_DOCS, preferred_element_type=jnp.fl...  113 us
    reduce_sum x4, other arithmetic, local_sweeps(): s_w = lax.psum(jnp.sum(w_loc, axis=0), 'row')  72.1 us
    psum x4, blocking collectives, local_sweeps(): s_h = lax.psum(jnp.sum(h_loc, axis=1), 'col')  52.4 us
    psum x4, blocking collectives, local_sweeps(): s_w = lax.psum(jnp.sum(w_loc, axis=0), 'row')  34.7 us
  transfers between devices with their start and end apart: 8, of which 8 were waited for; matrix products, arithmetic and copies ran while one was open for 0% of the time, Pallas kernels for 0%

commit v1 on v0

v1 whole, which is shorter than its diff:
```python
import functools

import jax
import jax.numpy as jnp
from jax import lax
from jax.experimental import pallas as pl
from jax.experimental.pallas import tpu as pltpu
from jax.sharding import PartitionSpec as P

SWEEPS = 4
EPS = 1e-6
RING = 4
SUBS = 2
BLK = 512
EW = 32
MESH = pl.DeviceIdType.MESH
F32 = jnp.float32
BF = jnp.bfloat16
CONTRACT_LAST = (((1,), (1,)), ((), ()))
CONTRACT_FIRST = (((0,), (0,)), ((), ()))


def mult(v, m):
    return pl.multiple_of(v, m)


def kernel(c_hbm, wb_hbm, hb_hbm, w0_hbm, h0_hbm, w_out, h_out,
           cv, wb, hb, wf, hf, wacc, hacc, wring, hring, wst, hst, d2d, sbuf, srecv, sfin,
           ld_sem, wr_s, wr_r, hr_s, hr_r, d2_s, d2_r, ag_s, ag_r, pg_s, pg_r, ss_s, ss_r):
    col = lax.axis_index("col")
    y = lax.axis_index("row")
    x, c = col // 2, lax.rem(col, 2)
    d = 1 - 2 * c
    docs, topics = wb.shape
    words = hb.shape[0]
    sw = docs // (2 * RING)
    sh = words // RING

    def mod(v):
        return lax.rem(v + 4 * RING, RING)

    def xdev(delta):
        return {"col": mod(x + delta) * 2 + c}

    def ydev(delta):
        return {"row": mod(y + delta)}

    partner = {"col": x * 2 + (1 - c)}

    def remote(src, dst, s_sem, r_sem, dev):
        return pltpu.make_async_remote_copy(src_ref=src, dst_ref=dst, send_sem=s_sem, recv_sem=r_sem,
                                            device_id=dev, device_id_type=MESH)

    barrier = pltpu.get_barrier_semaphore()
    for o in range(1, RING):
        pl.semaphore_signal(barrier, inc=1, device_id=xdev(o), device_id_type=MESH)
        pl.semaphore_signal(barrier, inc=1, device_id=ydev(o), device_id_type=MESH)
    pl.semaphore_signal(barrier, inc=1, device_id=partner, device_id_type=MESH)

    def wrows(k, h):
        return pl.ds(mult((k * 2 + h) * sw, sw), sw)

    def hrows(k):
        return pl.ds(mult(k * sh, sh), sh)

    loads = [
        pltpu.make_async_copy(hb_hbm, hb, ld_sem.at[0]),
        pltpu.make_async_copy(wb_hbm, wb, ld_sem.at[1]),
        pltpu.make_async_copy(c_hbm, cv, ld_sem.at[2]),
        pltpu.make_async_copy(w0_hbm.at[wrows(x, c)], wf, ld_sem.at[3]),
        pltpu.make_async_copy(h0_hbm.at[hrows(y)], hf, ld_sem.at[4]),
    ]
    for cp in loads:
        cp.start()
    pl.semaphore_wait(barrier, 2 * (RING - 1) + 1)
    for cp in loads:
        cp.wait()

    class Gather:
        def __init__(self, buf, own, slot, is_w):
            self.buf, self.own, self.slot, self.is_w = buf, own, slot, is_w
            self.p = x if is_w else y
            self.dev = xdev if is_w else ydev

        def rows(self, k, h):
            return wrows(k, h) if self.is_w else hrows(k)

        def ring(self, i):
            k = self.p if i < 2 else mod(self.p - d)
            dst = self.buf.at[self.rows(k, c)]
            src = self.own if (i < 2 and self.own is not None) else dst
            return remote(src, dst, ag_s.at[self.slot, i], ag_r.at[self.slot, i], self.dev(-d if i == 1 else d))

        def ring_in(self, i):
            k = mod(self.p + (-d, d, -2 * d)[i])
            dst = self.buf.at[self.rows(k, c)]
            return remote(dst, dst, ag_s.at[self.slot, i], ag_r.at[self.slot, i], self.dev(d))

        def pair(self, i):
            k = mod(self.p + (0, -d, d, 2)[i])
            dst = self.buf.at[self.rows(k, c)]
            src = self.own if (i == 0 and self.own is not None) else dst
            return remote(src, dst, pg_s.at[self.slot, i], pg_r.at[self.slot, i], partner)

        def pair_in(self, i):
            k = mod(self.p + (0, d, -d, 2)[i])
            dst = self.buf.at[self.rows(k, 1 - c)]
            return remote(dst, dst, pg_s.at[self.slot, i], pg_r.at[self.slot, i], partner)

        def start(self):
            self.ring(0).start()
            self.ring(1).start()
            if self.is_w:
                self.pair(0).start()

        def got(self, i):
            self.ring_in(i).wait_recv()
            if i == 0:
                self.ring(2).start()
            if self.is_w:
                self.pair(i + 1).start()

        def got_pair(self, i):
            if self.is_w:
                self.pair_in(i).wait_recv()

        def sent(self):
            for i in range(3):
                self.ring(i).wait_send()
            if self.is_w:
                for i in range(4):
                    self.pair(i).wait_send()

    wag = Gather(wb, None, 0, True)
    hag = Gather(hb, None, 1, False)
    wfin = Gather(w_out, wf, 2, True)
    hfin = Gather(h_out, hf, 3, False)

    class Sums:
        def __init__(self, role):
            self.r = role

        def copies(self, stage):
            r = self.r
            if stage == 0:
                return [remote(sbuf.at[r, 0], srecv.at[r, 0], ss_s.at[r, 0], ss_r.at[r, 0], partner)]
            dev = xdev if stage == 1 else ydev
            base = 1 if stage == 1 else RING
            return [remote(sbuf.at[r, stage], srecv.at[r, base + o - 1], ss_s.at[r, base + o - 1],
                           ss_r.at[r, base + o - 1], dev(o)) for o in range(1, RING)]

        def start(self, value):
            sbuf[self.r, 0] = value
            for cp in self.copies(0):
                cp.start()

        def step(self, stage):
            r = self.r
            cps = self.copies(stage - 1)
            total = sbuf[r, stage - 1]
            base = (0, 1, RING)[stage - 1]
            for i, cp in enumerate(cps):
                cp.wait_recv()
                total = total + srecv[r, base + i]
            for cp in cps:
                cp.wait_send()
            if stage < 3:
                sbuf[r, stage] = total
                for cp in self.copies(stage):
                    cp.start()
            else:
                sfin[r] = jnp.broadcast_to(jnp.sum(total, axis=0, keepdims=True), (8, topics))

    wsum, hsum = Sums(0), Sums(1)

    def colsum(ref):
        n = ref.shape[0]

        def body(i, tot):
            return tot + ref[pl.ds(mult(i * 8, 8), 8), :]

        return lax.fori_loop(0, n // 8, body, jnp.zeros((8, topics), F32), unroll=4)

    def w_part(rows, kk, width, first, dst_rows):
        cols = pl.ds(mult(kk * width, width), width)
        hk = hb[cols, :]
        z = lax.dot_general(wb[rows, :], hk, CONTRACT_LAST, preferred_element_type=F32)
        q = (cv[rows, cols].astype(F32) / (z + EPS)).astype(BF)
        a = jnp.dot(q, hk, preferred_element_type=F32)
        if first:
            wacc[dst_rows, :] = a
        else:
            wacc[dst_rows, :] += a

    def w_unit(s, kk, width, first):
        ko, kp = mod(x - (1 + s) * d), mod(x + (1 + s) * d)
        r_own, r_par = (ko * 2 + c) * sw, (kp * 2 + 1 - c) * sw
        per = sw // BLK

        @pl.loop(0, 2 * per)
        def _(i):
            base = jnp.where(i < per, r_own, r_par - sw)
            w_part(pl.ds(mult(base + i * BLK, BLK), BLK), kk, width, first, pl.ds(mult(i * BLK, BLK), BLK))

    def h_part(docs0, words_k, acc, first):
        rows = pl.ds(mult(docs0, BLK), BLK)
        cols = hrows(words_k)
        z = lax.dot_general(wb[rows, :], hb[cols, :], CONTRACT_LAST, preferred_element_type=F32)
        q = (cv[rows, cols].astype(F32) / (z + EPS)).astype(BF)
        a = lax.dot_general(q, wb[rows, :], CONTRACT_FIRST, preferred_element_type=F32)
        if first:
            acc[...] = a
        else:
            acc[...] += a

    def ring_out(ring, stage, s, i, rows_n, s_sem, r_sem, dev, from_stage):
        n = rows_n // SUBS
        rows = pl.ds(i * n, n)
        src = stage.at[rows] if from_stage else ring.at[s - 1, rows]
        return remote(src, ring.at[s, rows], s_sem.at[s, i], r_sem.at[s, i], dev)

    def d2d_copy(s):
        slot = lax.rem(s, 2)
        return remote(wacc.at[pl.ds(sw, sw)], d2d.at[slot], d2_s.at[slot], d2_r.at[slot], partner)

    def w_sweep(t):
        dev = xdev(d)
        p = y
        order = (p, mod(p - d), mod(p + d), mod(p + 2))
        w_unit(0, order[0], sh, True)

        @pl.when(t > 0)
        def _():
            hag.got(0)
            hag.got(1)

        hsum.step(1)
        w_unit(0, order[1], sh, False)
        w_unit(0, order[2], sh, False)
        hsum.step(2)

        @pl.when(t > 0)
        def _():
            hag.got(2)

        w_unit(0, order[3], sh, False)

        @pl.when(t > 0)
        def _():
            hag.sent()

        d2d_copy(0).start()
        d2d_copy(0).wait_recv()
        n = sw // SUBS
        for i in range(SUBS):
            @pl.loop(0, n // EW)
            def _(b):
                rows = pl.ds(mult(i * n + b * EW, EW), EW)
                wst[rows, :] = wacc[rows, :] + d2d[0, rows, :]
            ring_out(wring, wst, 0, i, sw, wr_s, wr_r, dev, True).start()
        hsum.step(3)
        d2d_copy(0).wait_send()

        @pl.loop(1, RING - 1)
        def _(s):
            w_unit(s, 0, words, True)
            d2d_copy(s).start()
            d2d_copy(s).wait_recv()
            slot = lax.rem(s, 2)
            for i in range(SUBS):
                ring_out(wring, wst, s - 1, i, sw, wr_s, wr_r, dev, True).wait_recv()

                @pl.loop(0, n // EW)
                def _(b):
                    rows = pl.ds(mult(i * n + b * EW, EW), EW)
                    wring[s - 1, rows, :] = wring[s - 1, rows, :] + (wacc[rows, :] + d2d[slot, rows, :])
                ring_out(wring, wst, s, i, sw, wr_s, wr_r, dev, False).start()
            d2d_copy(s).wait_send()

        s = RING - 1
        w_unit(s, 0, words, True)
        d2d_copy(s).start()
        d2d_copy(s).wait_recv()
        own = (x * 2 + c) * sw
        tot = jnp.zeros((8, topics), F32)
        for i in range(SUBS):
            ring_out(wring, wst, s - 1, i, sw, wr_s, wr_r, dev, False).wait_recv()

            def body(b, tot):
                r0 = mult(i * n + b * 16, 16)
                rows = pl.ds(r0, 16)
                a = wring[s - 1, rows, :] + (wacc[rows, :] + d2d[s % 2, rows, :])
                new = wf[rows, :] * a / jnp.concatenate([sfin[1], sfin[1]], axis=0)
                wf[rows, :] = new
                wb[pl.ds(mult(own + r0, 16), 16), :] = new.astype(BF)
                return tot + (new[:8] + new[8:])
            tot = lax.fori_loop(0, n // 16, body, tot)
        for ss in range(RING - 1):
            for i in range(SUBS):
                ring_out(wring, wst, ss, i, sw, wr_s, wr_r, dev, ss == 0).wait_send()
        d2d_copy(s).wait_send()
        wag.start()
        wsum.start(tot)

    def h_chunk(k, words_k, acc, first):
        per = 2 * sw // BLK
        base = k * 2 * sw
        if first:
            h_part(base, words_k, acc, True)

        @pl.loop(1 if first else 0, per)
        def _(i):
            h_part(base + i * BLK, words_k, acc, False)

    def h_sweep(t):
        dev = ydev(d)
        k0 = mod(y - d)
        n = sh // SUBS
        wag.got_pair(0)
        h_chunk(x, k0, hst, True)
        wsum.step(1)
        wag.got(0)
        wag.got(1)
        wag.got_pair(2)
        h_chunk(mod(x - d), k0, hst, False)
        wag.got_pair(1)
        h_chunk(mod(x + d), k0, hst, False)
        wsum.step(2)
        wag.got(2)
        wag.got_pair(3)
        h_chunk(mod(x + 2), k0, hst, False)
        wag.sent()
        for i in range(SUBS):
            ring_out(hring, hst, 0, i, sh, hr_s, hr_r, dev, True).start()

        @pl.when(t == SWEEPS - 1)
        def _():
            wfin.start()
            pltpu.make_async_copy(wf, w_out.at[wrows(x, c)], ld_sem.at[0]).start()

        wsum.step(3)

        @pl.loop(1, RING - 1)
        def _(s):
            k = mod(y - (1 + s) * d)
            h_part(0, k, hacc, True)

            @pl.loop(1, docs // BLK)
            def _(b):
                h_part(b * BLK, k, hacc, False)
            for i in range(SUBS):
                ring_out(hring, hst, s - 1, i, sh, hr_s, hr_r, dev, True).wait_recv()

                @pl.loop(0, n // EW)
                def _(b):
                    rows = pl.ds(mult(i * n + b * EW, EW), EW)
                    hring[s - 1, rows, :] = hring[s - 1, rows, :] + hacc[rows, :]
                ring_out(hring, hst, s, i, sh, hr_s, hr_r, dev, False).start()

        s = RING - 1
        h_part(0, y, hacc, True)

        @pl.loop(1, docs // BLK)
        def _(b):
            h_part(b * BLK, y, hacc, False)
        tot = jnp.zeros((8, topics), F32)
        for i in range(SUBS):
            ring_out(hring, hst, s - 1, i, sh, hr_s, hr_r, dev, False).wait_recv()

            def body(b, tot):
                r0 = mult(i * n + b * 16, 16)
                rows = pl.ds(r0, 16)
                a = hring[s - 1, rows, :] + hacc[rows, :]
                new = hf[rows, :] * a / jnp.concatenate([sfin[0], sfin[0]], axis=0)
                hf[rows, :] = new
                hb[pl.ds(mult(y * sh + r0, 16), 16), :] = new.astype(BF)
                return tot + (new[:8] + new[8:])
            tot = lax.fori_loop(0, n // 16, body, tot)
        for ss in range(RING - 1):
            for i in range(SUBS):
                ring_out(hring, hst, ss, i, sh, hr_s, hr_r, dev, ss == 0).wait_send()

        @pl.when(t < SWEEPS - 1)
        def _():
            hag.start()
            hsum.start(tot)

    hsum.start(colsum(hf))

    @pl.loop(0, SWEEPS)
    def _(t):
        w_sweep(t)
        h_sweep(t)

    hfin.start()
    hlocal = pltpu.make_async_copy(hf, h_out.at[hrows(y)], ld_sem.at[1])
    hlocal.start()
    wfin.got(0)
    wfin.got(1)
    hfin.got(0)
    hfin.got(1)
    wfin.got(2)
    hfin.got(2)
    for i in range(4):
        wfin.got_pair(i)
    wfin.sent()
    hfin.sent()
    hlocal.wait()
    pltpu.make_async_copy(wf, w_out.at[wrows(x, c)], ld_sem.at[0]).wait()


def local(c_blk, w_loc, h_loc):
    docs, words = c_blk.shape
    topics = w_loc.shape[1]
    ht = h_loc.T
    sw, sh = docs // (2 * RING), words // RING
    dma = pltpu.SemaphoreType.DMA
    w_out, h_out = pl.pallas_call(
        kernel,
        out_shape=(jax.ShapeDtypeStruct((docs, topics), F32), jax.ShapeDtypeStruct((words, topics), F32)),
        in_specs=[pl.BlockSpec(memory_space=pl.ANY)] * 5,
        out_specs=(pl.BlockSpec(memory_space=pl.ANY), pl.BlockSpec(memory_space=pl.ANY)),
        scratch_shapes=[
            pltpu.VMEM((docs, words), BF),
            pltpu.VMEM((docs, topics), BF),
            pltpu.VMEM((words, topics), BF),
            pltpu.VMEM((sw, topics), F32),
            pltpu.VMEM((sh, topics), F32),
            pltpu.VMEM((2 * sw, topics), F32),
            pltpu.VMEM((sh, topics), F32),
            pltpu.VMEM((RING - 1, sw, topics), F32),
            pltpu.VMEM((RING - 1, sh, topics), F32),
            pltpu.VMEM((sw, topics), F32),
            pltpu.VMEM((sh, topics), F32),
            pltpu.VMEM((2, sw, topics), F32),
            pltpu.VMEM((2, 3, 8, topics), F32),
            pltpu.VMEM((2, 2 * RING - 1, 8, topics), F32),
            pltpu.VMEM((2, 8, topics), F32),
            dma((5,)),
            dma((RING - 1, SUBS)), dma((RING - 1, SUBS)),
            dma((RING - 1, SUBS)), dma((RING - 1, SUBS)),
            dma((2,)), dma((2,)),
            dma((4, 3)), dma((4, 3)),
            dma((4, 4)), dma((4, 4)),
            dma((2, 2 * RING - 1)), dma((2, 2 * RING - 1)),
        ],
        compiler_params=pltpu.CompilerParams(collective_id=0, has_side_effects=True,
                                             vmem_limit_bytes=63 * 1024 * 1024),
    )(c_blk, w_loc.astype(BF), ht.astype(BF), w_loc, ht)
    return w_out, h_out.T


def solution(mesh):
    spec_c = P(('part', 'row'), 'col')
    spec_w = P(('part', 'row'), None)
    spec_h = P(None, ('part', 'col'))
    return jax.shard_map(local, mesh=mesh, in_specs=(spec_c, spec_w, spec_h), out_specs=(spec_w, spec_h), check_vma=False)
```

time: 1420 us -> 792 us (0.56)
  waiting for transfers between devices: 976 us -> 0 us
  Pallas kernels: 0 us -> 755 us
  matrix products: 231 us -> 0 us
  blocking collectives: 87.1 us -> 0 us
  other arithmetic: 99.2 us -> 12.9 us
  local copies, waits for them, and re-layouts: 0 us -> 22.7 us
    psum x8 -> x0, waiting for transfers between devices: 976 us -> none  [the longest x4 658 us: local_sweeps(): lax.psum(lax.dot_general(q_blk, h_bf, CONTRACT_WORDS, preferred_element_t...]
    pallas_call x0 -> x1, Pallas kernels: none -> 755 us  [local(): pl.pallas_call(kernel, out_shape=(jax.ShapeDtypeStruct((docs, topics), F3...]
    dot_general x8 -> x0, matrix products: 231 us -> none  [the longest x4 118 us: local_sweeps(): lax.dot_general(q_blk, h_bf, CONTRACT_WORDS, preferred_element_type=jnp.f...]
    reduce_sum x8 -> x0, other arithmetic: 92.5 us -> none  [the longest x4 72.1 us: local_sweeps(): s_w = lax.psum(jnp.sum(w_loc, axis=0), 'row')]
    psum x8 -> x0, blocking collectives: 87.1 us -> none  [the longest x4 52.4 us: local_sweeps(): s_h = lax.psum(jnp.sum(h_loc, axis=1), 'col')]
    unnamed x0 -> x3, local copies, waits for them, and re-layouts: none -> 22.7 us
  transfers between devices with their start and end apart: 8 -> 0, of which waited for: 8 -> 0; matrix products, arithmetic and copies ran while one was open for 0% -> 0% of each run, Pallas kernels for 0% -> 0%
where the time goes in v1:
time: 792 us; the launch traced here: 791 us
  Pallas kernels  755 us (95%)
  local copies, waits for them, and re-layouts  22.7 us (3%)
  other arithmetic  12.9 us (2%)
    pallas_call x1, Pallas kernels, local(): pl.pallas_call(kernel, out_shape=(jax.ShapeDtypeStruct((docs, topics), F3...  755 us
    unnamed x3, local copies, waits for them, and re-layouts  22.7 us

profile of v1, /device:TPU:97, one launch (start us, length us, event | category | flops | bytes accessed | tf_op | source)
XLA Modules:
  0.0 791.2 jit_solution(14293604659213780164)
XLA Ops:
  0.6 5.3 copy.5
  6.0 3.8 bitcast_convert_fusion.hb_hbm
  9.8 9.1 %convert_element_type.6.wb_hbm = bf16[4096,1024]{1,0:T(8,128)(2,1)} convert(f32[4096,1024]{1,0:T(8,128)} %w0_hbm.1) | non-fusion elementwise | flops 4194304 | bytes 25165824 | tf_op jit(solution)/shard_map/convert_element_type | solution.py:449
  18.9 755.0 %shard_map.50 = (f32[4096,1024]{1,0:T(8,128)}, f32[1024,1024]{1,0:T(8,128)}) custom-call(bf16[4096,1024]{1,0:T(8,128)(2,1)} %c_hbm.1, bf16[4096,1024]{1,0:T(8,128)(2,1)} %convert_element_type.6.wb_hbm, bf16[1024,1024]{1,0:T(8,128)(2,1)} %bitcast_convert_fusion.hb_hbm, f32[4096,1024]{1,0:T(8,128)} %w0_hbm.1, f32[1024,1024]{1,0:T(8,128)} %bitcast.3), custom_call_target="tpu_custom_call" | custom-call | tf_op jit(solution)/shard_map/pallas_call | solution.py:418
  773.9 5.3 copy.6
  779.3 12.0 %copy.8 = f32[4096,1024]{1,0:T(8,128)} copy(f32[4096,1024]{1,0:T(8,128)} %get-tuple-element.10) | data formatting | bytes 33554432

commit v2 on v0

v2 whole, which is shorter than its diff:
```python
import functools

import jax
import jax.numpy as jnp
from jax import lax
from jax.experimental import pallas as pl
from jax.experimental.pallas import tpu as pltpu
from jax.sharding import PartitionSpec as P

SWEEPS = 4
EPS = 1e-6
RING = 4
SUBS = 2
BLK = 512
EW = 32
ORDER = ((1, 0), (3, 0), (0, 1), (0, 3), (1, 1), (3, 3), (1, 3), (3, 1),
         (2, 0), (0, 2), (2, 1), (1, 2), (2, 3), (3, 2), (2, 2))
MESH = pl.DeviceIdType.MESH
F32 = jnp.float32
BF = jnp.bfloat16
CONTRACT_LAST = (((1,), (1,)), ((), ()))
CONTRACT_FIRST = (((0,), (0,)), ((), ()))


def mult(v, m):
    return pl.multiple_of(v, m)


def kernel(c_hbm, w0_hbm, h0_hbm, w_out, h_out,
           cv, wb, hb, wf, hf, wacc, hacc, wring, hring, wst, hst, d2d, sbuf, srecv, sfin,
           ld_sem, c_s, c_r, wr_s, wr_r, hr_s, hr_r, d2_s, d2_r, ag_s, ag_r, pg_s, pg_r, ss_s, ss_r):
    col = lax.axis_index("col")
    y = lax.axis_index("row")
    x, c = col // 2, lax.rem(col, 2)
    d = 1 - 2 * c
    _, docs, topics = wb.shape
    words = hb.shape[1]
    sw = docs // (2 * RING)
    sh = words // RING

    def mod(v):
        return lax.rem(v + 4 * RING, RING)

    def xdev(delta):
        return {"col": mod(x + delta) * 2 + c}

    def ydev(delta):
        return {"row": mod(y + delta)}

    def xydev(dx, dy):
        return {"row": mod(y + dy), "col": mod(x + dx) * 2 + c}

    partner = {"col": x * 2 + (1 - c)}
    wpos, hpos = (x, y), (y, x)
    wdev, hdev = (xdev, ydev), (ydev, xdev)

    def remote(src, dst, s_sem, r_sem, dev):
        return pltpu.make_async_remote_copy(src_ref=src, dst_ref=dst, send_sem=s_sem, recv_sem=r_sem,
                                            device_id=dev, device_id_type=MESH)

    barrier = pltpu.get_barrier_semaphore()
    for dx, dy in ORDER:
        pl.semaphore_signal(barrier, inc=1, device_id=xydev(dx, dy), device_id_type=MESH)
    pl.semaphore_signal(barrier, inc=1, device_id=partner, device_id_type=MESH)

    def wrows(k, h, base=0):
        return pl.ds(mult((k * 2 + h) * sw + base, sw), sw)

    def hrows(k):
        return pl.ds(mult(k * sh, sh), sh)

    def crows(k, base=0):
        return pl.ds(mult(k * 2 * sw + base, 2 * sw), 2 * sw)

    def hblock(b):
        return hring.at[b // (RING - 1), b % (RING - 1)]

    def wload(b):
        return pltpu.make_async_copy(w0_hbm.at[crows(b)], wacc.at[b % 2], ld_sem.at[9 + b])

    loads = [
        pltpu.make_async_copy(w0_hbm.at[wrows(x, c, docs)], wf.at[1], ld_sem.at[0]),
        pltpu.make_async_copy(w0_hbm.at[wrows(x, c)], wf.at[0], ld_sem.at[1]),
        pltpu.make_async_copy(c_hbm.at[pl.ds(0, docs)], cv.at[0], ld_sem.at[2]),
        pltpu.make_async_copy(c_hbm.at[crows(x, docs), hrows(y)], cv.at[1, crows(y), hrows(x)], ld_sem.at[3]),
    ]
    hloads = [pltpu.make_async_copy(h0_hbm.at[hrows(b)], hblock(b), ld_sem.at[4 + b]) for b in range(topics // sh)]
    for cp in hloads + loads + [wload(0), wload(1)]:
        cp.start()

    def c_move(dx, dy):
        return remote(c_hbm.at[crows(mod(x + dx), docs), hrows(mod(y + dy))], cv.at[1, crows(y), hrows(x)],
                      c_s.at[dx, dy], c_r.at[dx, dy], xydev(dx, dy))

    def c_in(dx, dy):
        dst = cv.at[1, crows(mod(y - dy)), hrows(mod(x - dx))]
        return remote(dst, dst, c_s.at[dx, dy], c_r.at[dx, dy], xydev(dx, dy))

    def piece(rows, j):
        n = rows.size // SUBS
        return pl.ds(mult(rows.start + j * n, n), n)

    class Gather:
        def __init__(self, buf, own, slot, pos, dev, rows, is_w):
            self.buf, self.own, self.slot, self.is_w = buf, own, slot, is_w
            self.p, self.dev, self.rows = pos, dev, rows

        def make(self, k, h, j, own, s_sem, r_sem, i, dev):
            rows = self.rows(k, h)
            dst = self.buf.at[piece(rows, j)]
            src = dst
            if own and self.own is not None:
                n = rows.size // SUBS
                src = self.own.at[pl.ds(j * n, n)]
            return remote(src, dst, s_sem.at[self.slot, i, j], r_sem.at[self.slot, i, j], dev)

        def ring(self, i, j):
            k = self.p if i < 2 else mod(self.p - d)
            return self.make(k, c, j, i < 2, ag_s, ag_r, i, self.dev(-d if i == 1 else d))

        def ring_in(self, i, j):
            k = mod(self.p + (-d, d, -2 * d)[i])
            return self.make(k, c, j, False, ag_s, ag_r, i, self.dev(d))

        def pair(self, i, j):
            k = mod(self.p + (0, -d, d, 2)[i])
            return self.make(k, c, j, i == 0, pg_s, pg_r, i, partner)

        def pair_in(self, i, j):
            k = mod(self.p + (0, d, -d, 2)[i])
            return self.make(k, 1 - c, j, False, pg_s, pg_r, i, partner)

        def start(self, j):
            self.ring(0, j).start()
            self.ring(1, j).start()
            if self.is_w:
                self.pair(0, j).start()

        def got(self, i, j):
            self.ring_in(i, j).wait_recv()
            if i == 0:
                self.ring(2, j).start()
            if self.is_w:
                self.pair(i + 1, j).start()

        def got_pair(self, i):
            if self.is_w:
                for j in range(SUBS):
                    self.pair_in(i, j).wait_recv()

        def sent(self):
            for j in range(SUBS):
                for i in range(3):
                    self.ring(i, j).wait_send()
                if self.is_w:
                    for i in range(4):
                        self.pair(i, j).wait_send()

    def got_near(gathers):
        for j in range(SUBS):
            for i in range(2):
                for ga in gathers:
                    ga.got(i, j)

    def got_far(gathers):
        for j in range(SUBS):
            for ga in gathers:
                ga.got(2, j)

    wag = [Gather(wb.at[g], None, g, wpos[g], wdev[g], wrows, True) for g in range(2)]
    hag = [Gather(hb.at[g], None, 2 + g, hpos[g], hdev[g], lambda k, h: hrows(k), False) for g in range(2)]
    wfin = [Gather(w_out, wf.at[g], 4 + g, x, xdev, functools.partial(wrows, base=g * docs), True) for g in range(2)]
    hfin = Gather(h_out, hf, 6, y, ydev, lambda k, h: hrows(k), False)

    class Sums:
        def __init__(self, role):
            self.r = role

        def copies(self, stage):
            r = self.r
            if stage == 0:
                return [remote(sbuf.at[r, 0], srecv.at[r, 0], ss_s.at[r, 0], ss_r.at[r, 0], partner)]
            dev = xdev if stage == 1 else ydev
            base = 1 if stage == 1 else RING
            return [remote(sbuf.at[r, stage], srecv.at[r, base + o - 1], ss_s.at[r, base + o - 1],
                           ss_r.at[r, base + o - 1], dev(o)) for o in range(1, RING)]

        def start(self, value):
            sbuf[self.r, 0] = value
            for cp in self.copies(0):
                cp.start()

        def step(self, stage):
            r = self.r
            cps = self.copies(stage - 1)
            total = sbuf[r, stage - 1]
            base = (0, 1, RING)[stage - 1]
            for i, cp in enumerate(cps):
                cp.wait_recv()
                total = total + srecv[r, base + i]
            for cp in cps:
                cp.wait_send()
            if stage < 3:
                sbuf[r, stage] = total
                for cp in self.copies(stage):
                    cp.start()
            else:
                sfin[r] = jnp.broadcast_to(jnp.sum(total, axis=0, keepdims=True), (8, topics))

    wsum, hsum = Sums(0), Sums(1)

    def turn(k):
        for b in range(topics // sh):
            v = hblock(b)[:, hrows(k)].T
            tcols = pl.ds(b * sh, sh)
            hb[0, hrows(k), tcols] = v.astype(BF)

            @pl.when(k == y)
            def _():
                hf[:, tcols] = v
                hb[1, hrows(x), tcols] = v.astype(BF)

    for cp in hloads:
        cp.wait()
    turn(y)
    loads[0].wait()

    @pl.loop(0, sw // EW)
    def _(b):
        rows = pl.ds(mult(b * EW, EW), EW)
        wb[1, pl.ds(mult((y * 2 + c) * sw + b * EW, EW), EW), :] = wf[1, rows, :].astype(BF)

    pl.semaphore_wait(barrier, len(ORDER) + 1)
    for j in range(SUBS):
        hag[1].start(j)
        wag[1].start(j)
    for dx, dy in ORDER:
        c_move(dx, dy).start()
    for o in range(1, RING):
        turn(mod(y + o))
    for b in range(docs // (2 * sw)):
        wload(b).wait()

        @pl.loop(0, 2 * sw // EW)
        def _(e):
            wb[0, pl.ds(mult(b * 2 * sw + e * EW, EW), EW), :] = wacc[b % 2, pl.ds(mult(e * EW, EW), EW), :].astype(BF)
        if b + 2 < docs // (2 * sw):
            wload(b + 2).start()
    for cp in loads[1:]:
        cp.wait()

    def colsum(ref):
        n = ref.shape[0]

        def body(i, tot):
            return tot + ref[pl.ds(mult(i * 8, 8), 8), :]

        return lax.fori_loop(0, n // 8, body, jnp.zeros((8, topics), F32), unroll=4)

    def w_unit(g, s, kk, width, first, halves=(0, 1)):
        p = wpos[g]
        rows = (wrows(mod(p - (1 + s) * d), c), wrows(mod(p + (1 + s) * d), 1 - c))
        rows = [rows[h] for h in halves]
        dst = pl.ds(halves[0] * sw, len(halves) * sw)
        cols = pl.ds(mult(kk * width, width), width)
        hk = hb[g, cols, :]
        wx = jnp.concatenate([wb[g, r, :] for r in rows], axis=0)
        cx = jnp.concatenate([cv[g, r, cols] for r in rows], axis=0)
        z = lax.dot_general(wx, hk, CONTRACT_LAST, preferred_element_type=F32)
        q = (cx.astype(F32) / (z + EPS)).astype(BF)
        a = jnp.dot(q, hk, preferred_element_type=F32)
        if first:
            wacc[g, dst, :] = a
        else:
            wacc[g, dst, :] += a

    def h_part(g, docs0, words_k, acc, first):
        rows = pl.ds(mult(docs0, BLK), BLK)
        cols = hrows(words_k)
        z = lax.dot_general(wb[g, rows, :], hb[g, cols, :], CONTRACT_LAST, preferred_element_type=F32)
        q = (cv[g, rows, cols].astype(F32) / (z + EPS)).astype(BF)
        a = lax.dot_general(q, wb[g, rows, :], CONTRACT_FIRST, preferred_element_type=F32)
        if first:
            acc[g] = a
        else:
            acc[g] += a

    def ring_out(g, ring, stage, s, i, rows_n, s_sem, r_sem, dev, from_stage):
        n = rows_n // SUBS
        rows = pl.ds(i * n, n)
        src = stage.at[g, rows] if from_stage else ring.at[g, s - 1, rows]
        return remote(src, ring.at[g, s, rows], s_sem.at[g, s, i], r_sem.at[g, s, i], dev)

    def w_ring(g, s, i, from_stage):
        return ring_out(g, wring, wst, s, i, sw, wr_s, wr_r, wdev[g](d), from_stage)

    def h_ring(g, s, i, from_stage):
        return ring_out(g, hring, hst, s, i, sh, hr_s, hr_r, hdev[g](d), from_stage)

    def d2d_copy(g, s):
        slot = lax.rem(s, 2)
        return remote(wacc.at[g, pl.ds(sw, sw)], d2d.at[g, slot], d2_s.at[g, slot], d2_r.at[g, slot], partner)

    def w_sweep(t):
        n = sw // SUBS
        orders = [(p, mod(p - d), mod(p + d), mod(p + 2)) for p in hpos]

        @pl.when(t == 0)
        def _():
            got_near([hag[1], wag[1]])
            got_far([hag[1], wag[1]])
            for i in range(4):
                wag[1].got_pair(i)
            hag[1].sent()
            wag[1].sent()
            for dx, dy in ORDER:
                c_in(dx, dy).wait_recv()
                c_move(dx, dy).wait_send()

        for g in range(2):
            w_unit(g, 0, orders[g][0], sh, True)

        @pl.when(t > 0)
        def _():
            got_near(hag)

        hsum.step(1)
        for i in (1, 2):
            for g in range(2):
                w_unit(g, 0, orders[g][i], sh, False)
        hsum.step(2)

        @pl.when(t > 0)
        def _():
            got_far(hag)

        for g in range(2):
            w_unit(g, 0, orders[g][3], sh, False, (1,))
            d2d_copy(g, 0).start()
        for g in range(2):
            w_unit(g, 0, orders[g][3], sh, False, (0,))
        for g in range(2):
            d2d_copy(g, 0).wait_recv()
        for i in range(SUBS):
            for g in range(2):
                @pl.loop(0, n // EW)
                def _(b):
                    rows = pl.ds(mult(i * n + b * EW, EW), EW)
                    wst[g, rows, :] = wacc[g, rows, :] + d2d[g, 0, rows, :]
                w_ring(g, 0, i, True).start()

        @pl.when(t > 0)
        def _():
            for g in range(2):
                hag[g].sent()

        hsum.step(3)
        for g in range(2):
            d2d_copy(g, 0).wait_send()

        @pl.loop(1, RING)
        def _(s):
            for g in range(2):
                w_unit(g, s, 0, words, True)
                d2d_copy(g, s).start()
            slot = lax.rem(s, 2)
            for g in range(2):
                d2d_copy(g, s).wait_recv()

            @pl.when(s < RING - 1)
            def _():
                for i in range(SUBS):
                    for g in range(2):
                        w_ring(g, s - 1, i, True).wait_recv()

                        @pl.loop(0, n // EW)
                        def _(b):
                            rows = pl.ds(mult(i * n + b * EW, EW), EW)
                            wring[g, s - 1, rows, :] = wring[g, s - 1, rows, :] + (wacc[g, rows, :] + d2d[g, slot, rows, :])
                        w_ring(g, s, i, False).start()
            for g in range(2):
                d2d_copy(g, s).wait_send()

        s = RING - 1
        tot = jnp.zeros((8, topics), F32)
        for i in range(SUBS):
            for g in range(2):
                own = (wpos[g] * 2 + c) * sw
                w_ring(g, s - 1, i, False).wait_recv()

                def body(b, tot):
                    r0 = mult(i * n + b * 16, 16)
                    rows = pl.ds(r0, 16)
                    a = wring[g, s - 1, rows, :] + (wacc[g, rows, :] + d2d[g, s % 2, rows, :])
                    new = wf[g, rows, :] * a / jnp.concatenate([sfin[1], sfin[1]], axis=0)
                    wf[g, rows, :] = new
                    wb[g, pl.ds(mult(own + r0, 16), 16), :] = new.astype(BF)
                    return tot + (new[:8] + new[8:])
                tot = lax.fori_loop(0, n // 16, body, tot)
                wag[g].start(i)
        wsum.start(tot)
        for g in range(2):
            for ss in range(RING - 1):
                for i in range(SUBS):
                    w_ring(g, ss, i, ss == 0).wait_send()

    def h_sweep(t):
        n = sh // SUBS
        k0 = [mod(p - d) for p in hpos]

        def chunk(g, delta, first):
            h_part(g, mod(wpos[g] + delta) * BLK, k0[g], hst, first)

        for g in range(2):
            wag[g].got_pair(0)
            chunk(g, 0, True)
        wsum.step(1)
        got_near(wag)
        for g in range(2):
            wag[g].got_pair(2)
            chunk(g, -d, False)
        for g in range(2):
            wag[g].got_pair(1)
            chunk(g, d, False)
        wsum.step(2)
        got_far(wag)
        for g in range(2):
            wag[g].got_pair(3)
            chunk(g, 2, False)
            for i in range(SUBS):
                h_ring(g, 0, i, True).start()
        for g in range(2):
            wag[g].sent()
        wsum.step(3)

        @pl.loop(1, RING)
        def _(s):
            for g in range(2):
                k = mod(hpos[g] - (1 + s) * d)
                h_part(g, 0, k, hacc, True)

                @pl.loop(1, docs // BLK)
                def _(b):
                    h_part(g, b * BLK, k, hacc, False)

            @pl.when(s < RING - 1)
            def _():
                for i in range(SUBS):
                    for g in range(2):
                        h_ring(g, s - 1, i, True).wait_recv()

                        @pl.loop(0, n // EW)
                        def _(b):
                            rows = pl.ds(mult(i * n + b * EW, EW), EW)
                            hring[g, s - 1, rows, :] = hring[g, s - 1, rows, :] + hacc[g, rows, :]
                        h_ring(g, s, i, False).start()

        @pl.when(t == SWEEPS - 1)
        def _():
            for g in range(2):
                for j in range(SUBS):
                    wfin[g].start(j)
                wlocal(g).start()

        s = RING - 1
        tot = jnp.zeros((8, topics), F32)
        for i in range(SUBS):
            for g in range(2):
                h_ring(g, s - 1, i, False).wait_recv()

            def body(b, tot):
                r0 = mult(i * n + b * 16, 16)
                rows = pl.ds(r0, 16)
                a = (hring[0, s - 1, rows, :] + hacc[0, rows, :]) + (hring[1, s - 1, rows, :] + hacc[1, rows, :])
                new = hf[rows, :] * a / jnp.concatenate([sfin[0], sfin[0]], axis=0)
                hf[rows, :] = new
                for g in range(2):
                    hb[g, pl.ds(mult(hpos[g] * sh + r0, 16), 16), :] = new.astype(BF)
                return tot + (new[:8] + new[8:])
            tot = lax.fori_loop(0, n // 16, body, tot)

            @pl.when(t < SWEEPS - 1)
            def _():
                for g in range(2):
                    hag[g].start(i)

            @pl.when(t == SWEEPS - 1)
            def _():
                hfin.start(i)

        @pl.when(t < SWEEPS - 1)
        def _():
            hsum.start(tot)

        for g in range(2):
            for ss in range(RING - 1):
                for i in range(SUBS):
                    h_ring(g, ss, i, ss == 0).wait_send()

    def wlocal(g):
        return pltpu.make_async_copy(wf.at[g], w_out.at[wrows(x, c, g * docs)], ld_sem.at[g])

    hsum.start(colsum(hf))

    @pl.loop(0, SWEEPS)
    def _(t):
        w_sweep(t)
        h_sweep(t)

    hlocal = pltpu.make_async_copy(hf, h_out.at[hrows(y)], ld_sem.at[2])
    hlocal.start()
    got_near([hfin])
    got_near(wfin)
    got_far([hfin])
    got_far(wfin)
    for g in range(2):
        for i in range(4):
            wfin[g].got_pair(i)
        wfin[g].sent()
        wlocal(g).wait()
    hfin.sent()
    hlocal.wait()


def local(c_blk, w_loc, h_loc):
    docs, words = c_blk.shape
    topics = w_loc.shape[1]
    half = docs // 2
    sw, sh = half // (2 * RING), words // RING
    dma = pltpu.SemaphoreType.DMA
    w_out, h_out = pl.pallas_call(
        kernel,
        out_shape=(jax.ShapeDtypeStruct((docs, topics), F32), jax.ShapeDtypeStruct((words, topics), F32)),
        in_specs=[pl.BlockSpec(memory_space=pl.ANY)] * 3,
        out_specs=(pl.BlockSpec(memory_space=pl.ANY), pl.BlockSpec(memory_space=pl.ANY)),
        scratch_shapes=[
            pltpu.VMEM((2, half, words), BF),
            pltpu.VMEM((2, half, topics), BF),
            pltpu.VMEM((2, words, topics), BF),
            pltpu.VMEM((2, sw, topics), F32),
            pltpu.VMEM((sh, topics), F32),
            pltpu.VMEM((2, 2 * sw, topics), F32),
            pltpu.VMEM((2, sh, topics), F32),
            pltpu.VMEM((2, RING - 1, sw, topics), F32),
            pltpu.VMEM((2, RING - 1, sh, topics), F32),
            pltpu.VMEM((2, sw, topics), F32),
            pltpu.VMEM((2, sh, topics), F32),
            pltpu.VMEM((2, 2, sw, topics), F32),
            pltpu.VMEM((2, 3, 8, topics), F32),
            pltpu.VMEM((2, 2 * RING - 1, 8, topics), F32),
            pltpu.VMEM((2, 8, topics), F32),
            dma((13,)),
            dma((RING, RING)), dma((RING, RING)),
            dma((2, RING - 1, SUBS)), dma((2, RING - 1, SUBS)),
            dma((2, RING - 1, SUBS)), dma((2, RING - 1, SUBS)),
            dma((2, 2)), dma((2, 2)),
            dma((7, 3, SUBS)), dma((7, 3, SUBS)),
            dma((7, 4, SUBS)), dma((7, 4, SUBS)),
            dma((2, 2 * RING - 1)), dma((2, 2 * RING - 1)),
        ],
        compiler_params=pltpu.CompilerParams(collective_id=0, has_side_effects=True,
                                             vmem_limit_bytes=63 * 1024 * 1024),
    )(c_blk, w_loc, h_loc)
    return w_out, h_out.T


def solution(mesh):
    spec_c = P(('part', 'row'), 'col')
    spec_w = P(('part', 'row'), None)
    spec_h = P(None, ('part', 'col'))
    return jax.shard_map(local, mesh=mesh, in_specs=(spec_c, spec_w, spec_h), out_specs=(spec_w, spec_h), check_vma=False)
```

time: 1420 us -> 650 us (0.46)
  waiting for transfers between devices: 976 us -> 0 us
  Pallas kernels: 0 us -> 632 us
  matrix products: 231 us -> 0 us
  other arithmetic: 99.2 us -> 0 us
  blocking collectives: 87.1 us -> 0 us
  local copies, waits for them, and re-layouts: 0 us -> 17.3 us
    psum x8 -> x0, waiting for transfers between devices: 976 us -> none  [the longest x4 658 us: local_sweeps(): lax.psum(lax.dot_general(q_blk, h_bf, CONTRACT_WORDS, preferred_element_t...]
    pallas_call x0 -> x1, Pallas kernels: none -> 632 us  [local(): pl.pallas_call(kernel, out_shape=(jax.ShapeDtypeStruct((docs, topics), F3...]
    dot_general x8 -> x0, matrix products: 231 us -> none  [the longest x4 118 us: local_sweeps(): lax.dot_general(q_blk, h_bf, CONTRACT_WORDS, preferred_element_type=jnp.f...]
    reduce_sum x8 -> x0, other arithmetic: 92.5 us -> none  [the longest x4 72.1 us: local_sweeps(): s_w = lax.psum(jnp.sum(w_loc, axis=0), 'row')]
    psum x8 -> x0, blocking collectives: 87.1 us -> none  [the longest x4 52.4 us: local_sweeps(): s_h = lax.psum(jnp.sum(h_loc, axis=1), 'col')]
    unnamed x0 -> x2, local copies, waits for them, and re-layouts: none -> 17.3 us
  transfers between devices with their start and end apart: 8 -> 0, of which waited for: 8 -> 0; matrix products, arithmetic and copies ran while one was open for 0% -> 0% of each run, Pallas kernels for 0% -> 0%
where the time goes in v2:
time: 650 us
  Pallas kernels  632 us (97%)
  local copies, waits for them, and re-layouts  17.3 us (3%)
    pallas_call x1, Pallas kernels, local(): pl.pallas_call(kernel, out_shape=(jax.ShapeDtypeStruct((docs, topics), F3...  632 us
    unnamed x2, local copies, waits for them, and re-layouts  17.3 us

profile of v2, /device:TPU:97, one launch (start us, length us, event | category | flops | bytes accessed | tf_op | source)
XLA Modules:
  0.0 649.6 jit_solution(16404825942315935788)
XLA Ops:
  0.6 631.6 %shard_map.50 = (f32[4096,1024]{1,0:T(8,128)}, f32[1024,1024]{1,0:T(8,128)}) custom-call(bf16[4096,1024]{1,0:T(8,128)(2,1)} %c_hbm.1, f32[4096,1024]{1,0:T(8,128)} %w0_hbm.1, f32[1024,1024]{1,0:T(8,128)} %h0_hbm.1), custom_call_target="tpu_custom_call" | custom-call | tf_op jit(solution)/shard_map/pallas_call | solution.py:531
  632.3 5.3 copy.5
  637.6 12.0 %copy.7 = f32[4096,1024]{1,0:T(8,128)} copy(f32[4096,1024]{1,0:T(8,128)} %get-tuple-element.10) | data formatting | bytes 33554432

commit v3 on v2

--- a/solution.py
+++ b/solution.py
@@ -13,8 +13,10 @@
 SUBS = 2
 BLK = 512
 EW = 32
-ORDER = ((1, 0), (3, 0), (0, 1), (0, 3), (1, 1), (3, 3), (1, 3), (3, 1),
-         (2, 0), (0, 2), (2, 1), (1, 2), (2, 3), (3, 2), (2, 2))
+C_FIRST = ((0, 1), (0, 3), (1, 1), (3, 3), (1, 3), (3, 1), (2, 1), (2, 3))
+C_NEXT = ((1, 2), (3, 2), (0, 2), (2, 2))
+C_LAST = ((1, 0), (3, 0), (2, 0))
+ORDER = C_FIRST + C_NEXT + C_LAST
 MESH = pl.DeviceIdType.MESH
 F32 = jnp.float32
 BF = jnp.bfloat16
@@ -220,6 +222,9 @@
                 hf[:, tcols] = v
                 hb[1, hrows(x), tcols] = v.astype(BF)
 
+    pl.semaphore_wait(barrier, len(ORDER) + 1)
+    for dx, dy in ORDER[:8]:
+        c_move(dx, dy).start()
     for cp in hloads:
         cp.wait()
     turn(y)
@@ -230,11 +235,10 @@
         rows = pl.ds(mult(b * EW, EW), EW)
         wb[1, pl.ds(mult((y * 2 + c) * sw + b * EW, EW), EW), :] = wf[1, rows, :].astype(BF)
 
-    pl.semaphore_wait(barrier, len(ORDER) + 1)
     for j in range(SUBS):
         hag[1].start(j)
         wag[1].start(j)
-    for dx, dy in ORDER:
+    for dx, dy in ORDER[8:]:
         c_move(dx, dy).start()
     for o in range(1, RING):
         turn(mod(y + o))
@@ -274,8 +278,8 @@
         else:
             wacc[g, dst, :] += a
 
-    def h_part(g, docs0, words_k, acc, first):
-        rows = pl.ds(mult(docs0, BLK), BLK)
+    def h_part(g, docs0, words_k, acc, first, blk=BLK):
+        rows = pl.ds(mult(docs0, blk), blk)
         cols = hrows(words_k)
         z = lax.dot_general(wb[g, rows, :], hb[g, cols, :], CONTRACT_LAST, preferred_element_type=F32)
         q = (cv[g, rows, cols].astype(F32) / (z + EPS)).astype(BF)
@@ -297,13 +301,17 @@
     def h_ring(g, s, i, from_stage):
         return ring_out(g, hring, hst, s, i, sh, hr_s, hr_r, hdev[g](d), from_stage)
 
-    def d2d_copy(g, s):
+    def d2d_copy(g, s, i):
         slot = lax.rem(s, 2)
-        return remote(wacc.at[g, pl.ds(sw, sw)], d2d.at[g, slot], d2_s.at[g, slot], d2_r.at[g, slot], partner)
+        n = sw // SUBS
+        return remote(wacc.at[g, pl.ds(sw + i * n, n)], d2d.at[g, slot, pl.ds(i * n, n)],
+                      d2_s.at[g, slot, i], d2_r.at[g, slot, i], partner)
 
     def w_sweep(t):
         n = sw // SUBS
         orders = [(p, mod(p - d), mod(p + d), mod(p + 2)) for p in hpos]
+
+        w_unit(0, 0, orders[0][0], sh, True)
 
         @pl.when(t == 0)
         def _():
@@ -313,12 +321,10 @@
                 wag[1].got_pair(i)
             hag[1].sent()
             wag[1].sent()
-            for dx, dy in ORDER:
+            for dx, dy in C_FIRST:
                 c_in(dx, dy).wait_recv()
-                c_move(dx, dy).wait_send()
-
-        for g in range(2):
-            w_unit(g, 0, orders[g][0], sh, True)
+
+        w_unit(1, 0, orders[1][0], sh, True)
 
         @pl.when(t > 0)
         def _():
@@ -336,13 +342,14 @@
 
         for g in range(2):
             w_unit(g, 0, orders[g][3], sh, False, (1,))
-            d2d_copy(g, 0).start()
+            for i in range(SUBS):
+                d2d_copy(g, 0, i).start()
         for g in range(2):
             w_unit(g, 0, orders[g][3], sh, False, (0,))
-        for g in range(2):
-            d2d_copy(g, 0).wait_recv()
         for i in range(SUBS):
             for g in range(2):
+                d2d_copy(g, 0, i).wait_recv()
+
                 @pl.loop(0, n // EW)
                 def _(b):
                     rows = pl.ds(mult(i * n + b * EW, EW), EW)
@@ -356,16 +363,31 @@
 
         hsum.step(3)
         for g in range(2):
-            d2d_copy(g, 0).wait_send()
+            for i in range(SUBS):
+                d2d_copy(g, 0, i).wait_send()
 
         @pl.loop(1, RING)
         def _(s):
             for g in range(2):
+                if g == 1:
+                    @pl.when(jnp.logical_and(t == 0, s == 1))
+                    def _():
+                        for dx, dy in C_NEXT:
+                            c_in(dx, dy).wait_recv()
+
+                    @pl.when(jnp.logical_and(t == 0, s == RING - 1))
+                    def _():
+                        for dx, dy in C_LAST:
+                            c_in(dx, dy).wait_recv()
+                        for dx, dy in ORDER:
+                            c_move(dx, dy).wait_send()
                 w_unit(g, s, 0, words, True)
-                d2d_copy(g, s).start()
+                for i in range(SUBS):
+                    d2d_copy(g, s, i).start()
             slot = lax.rem(s, 2)
             for g in range(2):
-                d2d_copy(g, s).wait_recv()
+                for i in range(SUBS):
+                    d2d_copy(g, s, i).wait_recv()
 
             @pl.when(s < RING - 1)
             def _():
@@ -379,7 +401,8 @@
                             wring[g, s - 1, rows, :] = wring[g, s - 1, rows, :] + (wacc[g, rows, :] + d2d[g, slot, rows, :])
                         w_ring(g, s, i, False).start()
             for g in range(2):
-                d2d_copy(g, s).wait_send()
+                for i in range(SUBS):
+                    d2d_copy(g, s, i).wait_send()
 
         s = RING - 1
         tot = jnp.zeros((8, topics), F32)
@@ -397,7 +420,16 @@
                     wb[g, pl.ds(mult(own + r0, 16), 16), :] = new.astype(BF)
                     return tot + (new[:8] + new[8:])
                 tot = lax.fori_loop(0, n // 16, body, tot)
-                wag[g].start(i)
+                if g == 0:
+                    @pl.when(t < SWEEPS - 1)
+                    def _():
+                        wag[0].start(i)
+
+                    @pl.when(t == SWEEPS - 1)
+                    def _():
+                        wfin[0].start(i)
+                else:
+                    wag[1].start(i)
         wsum.start(tot)
         for g in range(2):
             for ss in range(RING - 1):
@@ -411,26 +443,82 @@
         def chunk(g, delta, first):
             h_part(g, mod(wpos[g] + delta) * BLK, k0[g], hst, first)
 
-        for g in range(2):
-            wag[g].got_pair(0)
+        last = t == SWEEPS - 1
+
+        def fetch(delta, halves):
+            k = mod(x + delta)
+            cps = [pltpu.make_async_copy(w_out.at[wrows(k, h)], wring.at[0, i], ld_sem.at[2 + i])
+                   for i, h in enumerate(halves)]
+            for cp in cps:
+                cp.start()
+            for i, h in enumerate(halves):
+                cps[i].wait()
+
+                @pl.loop(0, sw // EW)
+                def _(e):
+                    rows = pl.ds(mult((k * 2 + h) * sw + e * EW, EW), EW)
+                    wb[0, rows, :] = wring[0, i, pl.ds(mult(e * EW, EW), EW), :].astype(BF)
+
+        def have(i, delta, halves):
+            @pl.when(jnp.logical_not(last))
+            def _():
+                wag[0].got_pair(i)
+
+            @pl.when(last)
+            def _():
+                wfin[0].got_pair(i)
+                fetch(delta, halves)
+
+        have(0, 0, (1 - c,))
+        wag[1].got_pair(0)
+        for g in range(2):
             chunk(g, 0, True)
         wsum.step(1)
-        got_near(wag)
-        for g in range(2):
-            wag[g].got_pair(2)
-            chunk(g, -d, False)
-        for g in range(2):
-            wag[g].got_pair(1)
-            chunk(g, d, False)
+
+        @pl.when(jnp.logical_not(last))
+        def _():
+            got_near(wag)
+
+        @pl.when(last)
+        def _():
+            got_near([wfin[0], wag[1]])
+
+        for i, delta in ((2, -d), (1, d)):
+            have(i, delta, (0, 1))
+            wag[1].got_pair(i)
+            for g in range(2):
+                chunk(g, delta, False)
         wsum.step(2)
-        got_far(wag)
-        for g in range(2):
-            wag[g].got_pair(3)
-            chunk(g, 2, False)
+
+        @pl.when(jnp.logical_not(last))
+        def _():
+            got_far(wag)
+
+        @pl.when(last)
+        def _():
+            got_far([wfin[0], wag[1]])
+
+        @pl.when(last)
+        def _():
+            fetch(2, (c,))
+
+        def far_half(g, h):
+            h_part(g, (mod(wpos[g] + 2) * 2 + h) * sw, k0[g], hst, False, sw)
+
+        for g in range(2):
+            far_half(g, c)
+        have(3, 2, (1 - c,))
+        wag[1].got_pair(3)
+        for g in range(2):
+            far_half(g, 1 - c)
             for i in range(SUBS):
                 h_ring(g, 0, i, True).start()
-        for g in range(2):
-            wag[g].sent()
+        wag[1].sent()
+
+        @pl.when(jnp.logical_not(last))
+        def _():
+            wag[0].sent()
+
         wsum.step(3)
 
         @pl.loop(1, RING)
@@ -457,9 +545,9 @@
 
         @pl.when(t == SWEEPS - 1)
         def _():
-            for g in range(2):
-                for j in range(SUBS):
-                    wfin[g].start(j)
+            for j in range(SUBS):
+                wfin[1].start(j)
+            for g in range(2):
                 wlocal(g).start()
 
         s = RING - 1
@@ -509,13 +597,12 @@
 
     hlocal = pltpu.make_async_copy(hf, h_out.at[hrows(y)], ld_sem.at[2])
     hlocal.start()
-    got_near([hfin])
-    got_near(wfin)
-    got_far([hfin])
-    got_far(wfin)
+    got_near([wfin[1], hfin])
+    got_far([wfin[1], hfin])
     for g in range(2):
-        for i in range(4):
-            wfin[g].got_pair(i)
+        if g == 1:
+            for i in range(4):
+                wfin[1].got_pair(i)
         wfin[g].sent()
         wlocal(g).wait()
     hfin.sent()
@@ -553,7 +640,7 @@
             dma((RING, RING)), dma((RING, RING)),
             dma((2, RING - 1, SUBS)), dma((2, RING - 1, SUBS)),
             dma((2, RING - 1, SUBS)), dma((2, RING - 1, SUBS)),
-            dma((2, 2)), dma((2, 2)),
+            dma((2, 2, SUBS)), dma((2, 2, SUBS)),
             dma((7, 3, SUBS)), dma((7, 3, SUBS)),
             dma((7, 4, SUBS)), dma((7, 4, SUBS)),
             dma((2, 2 * RING - 1)), dma((2, 2 * RING - 1)),

time: 650 us -> 614 us (0.945)
  Pallas kernels: 632 us -> 595 us
    pallas_call x1, Pallas kernels: 632 us -> 595 us  [local(): pl.pallas_call(kernel, out_shape=(jax.ShapeDtypeStruct((docs, topics), F3...]
where the time goes in v3:
time: 614 us; the launch traced here: 613 us
  Pallas kernels  595 us (97%)
  local copies, waits for them, and re-layouts  17.3 us (3%)
    pallas_call x1, Pallas kernels, local(): pl.pallas_call(kernel, out_shape=(jax.ShapeDtypeStruct((docs, topics), F3...  595 us
    unnamed x2, local copies, waits for them, and re-layouts  17.3 us

profile of v3, /device:TPU:97, one launch (start us, length us, event | category | flops | bytes accessed | tf_op | source)
XLA Modules:
  0.0 613.3 jit_solution(1314662277999982750)
XLA Ops:
  0.6 595.4 %shard_map.50 = (f32[4096,1024]{1,0:T(8,128)}, f32[1024,1024]{1,0:T(8,128)}) custom-call(bf16[4096,1024]{1,0:T(8,128)(2,1)} %c_hbm.1, f32[4096,1024]{1,0:T(8,128)} %w0_hbm.1, f32[1024,1024]{1,0:T(8,128)} %h0_hbm.1), custom_call_target="tpu_custom_call" | custom-call | tf_op jit(solution)/shard_map/pallas_call | solution.py:618
  596.0 5.3 copy.5
  601.4 12.0 %copy.7 = f32[4096,1024]{1,0:T(8,128)} copy(f32[4096,1024]{1,0:T(8,128)} %get-tuple-element.10) | data formatting | bytes 33554432

commit v4 on v3

--- a/solution.py
+++ b/solution.py
@@ -223,7 +223,7 @@
                 hb[1, hrows(x), tcols] = v.astype(BF)
 
     pl.semaphore_wait(barrier, len(ORDER) + 1)
-    for dx, dy in ORDER[:8]:
+    for dx, dy in C_FIRST:
         c_move(dx, dy).start()
     for cp in hloads:
         cp.wait()
@@ -238,8 +238,6 @@
     for j in range(SUBS):
         hag[1].start(j)
         wag[1].start(j)
-    for dx, dy in ORDER[8:]:
-        c_move(dx, dy).start()
     for o in range(1, RING):
         turn(mod(y + o))
     for b in range(docs // (2 * sw)):
@@ -316,6 +314,8 @@
         @pl.when(t == 0)
         def _():
             got_near([hag[1], wag[1]])
+            for dx, dy in C_NEXT + C_LAST:
+                c_move(dx, dy).start()
             got_far([hag[1], wag[1]])
             for i in range(4):
                 wag[1].got_pair(i)
@@ -334,8 +334,6 @@
         for i in (1, 2):
             for g in range(2):
                 w_unit(g, 0, orders[g][i], sh, False)
-        hsum.step(2)
-
         @pl.when(t > 0)
         def _():
             got_far(hag)
@@ -361,7 +359,7 @@
             for g in range(2):
                 hag[g].sent()
 
-        hsum.step(3)
+        hsum.step(2)
         for g in range(2):
             for i in range(SUBS):
                 d2d_copy(g, 0, i).wait_send()
@@ -404,6 +402,7 @@
                 for i in range(SUBS):
                     d2d_copy(g, s, i).wait_send()
 
+        hsum.step(3)
         s = RING - 1
         tot = jnp.zeros((8, topics), F32)
         for i in range(SUBS):
@@ -488,7 +487,6 @@
             wag[1].got_pair(i)
             for g in range(2):
                 chunk(g, delta, False)
-        wsum.step(2)
 
         @pl.when(jnp.logical_not(last))
         def _():
@@ -519,7 +517,7 @@
         def _():
             wag[0].sent()
 
-        wsum.step(3)
+        wsum.step(2)
 
         @pl.loop(1, RING)
         def _(s):
@@ -550,6 +548,7 @@
             for g in range(2):
                 wlocal(g).start()
 
+        wsum.step(3)
         s = RING - 1
         tot = jnp.zeros((8, topics), F32)
         for i in range(SUBS):

time: 614 us -> 608 us (level)
  no operation moved by 1% of the time
where the time goes in v4:
time: 608 us
  Pallas kernels  590 us (97%)
  local copies, waits for them, and re-layouts  17.3 us (3%)
    pallas_call x1, Pallas kernels, local(): pl.pallas_call(kernel, out_shape=(jax.ShapeDtypeStruct((docs, topics), F3...  590 us
    unnamed x2, local copies, waits for them, and re-layouts  17.3 us

profile of v4, /device:TPU:97, one launch (start us, length us, event | category | flops | bytes accessed | tf_op | source)
XLA Modules:
  0.0 607.6 jit_solution(4323301636392260984)
XLA Ops:
  0.6 589.6 %shard_map.50 = (f32[4096,1024]{1,0:T(8,128)}, f32[1024,1024]{1,0:T(8,128)}) custom-call(bf16[4096,1024]{1,0:T(8,128)(2,1)} %c_hbm.1, f32[4096,1024]{1,0:T(8,128)} %w0_hbm.1, f32[1024,1024]{1,0:T(8,128)} %h0_hbm.1), custom_call_target="tpu_custom_call" | custom-call | tf_op jit(solution)/shard_map/pallas_call | solution.py:617
  590.3 5.3 copy.5
  595.6 12.0 %copy.7 = f32[4096,1024]{1,0:T(8,128)} copy(f32[4096,1024]{1,0:T(8,128)} %get-tuple-element.10) | data formatting | bytes 33554432
